TPU v7x, 32 devices: a whole 2x2x4 slice. The times are simulated.
32 devices in a mesh: net: 4 (over y, x), line: 8 (over z, core).
Axes of the slice: x: 2, y: 2, z: 4, core: 2. Of those that a mesh axis runs over, the one named last changes fastest.
Arguments:
- conductance_inverse: float32 [4, 4096, 4096], P('net', 'line'), may hold values from -0.5 to 4.5, as said below
- prior_voltage: float32 [4, 96, 4096], P('net', None, 'line'), may hold values from -6 to 6
- sources: float32 [3, 4, 4096], P(None, 'net', 'line'), may hold values from -6 to 6
- fault_node: int32 [96], replicated, may hold values from 0 to 16383
- fault_conductance: float32 [96], replicated, may hold values from 0.5 to 4
- terminal_node: int32 [4, 3, 4096], P('net', None, 'line'), may hold values from 0 to 4095
- ownership: int32 [4, 4096], P('net', 'line'), may hold values from 0 to 1, as said below
- partner: int32 [4, 4096], P('net', 'line'), may hold values from 0 to 31, as said below
- delay_steps: int32 [4, 4096], P('net', 'line'), may hold values from 1 to 4, as said below
- surge_conductance: float32 [4, 4096], P('net', 'line'), may hold values from 0.2 to 1
- pole_wave: float32 [4, 6, 4096], P('net', None, 'line'), may hold values from 0.2 to 0.95
- residue_wave: float32 [4, 6, 3, 3, 4096], P('net', None, None, None, 'line'), may hold values from -1 to 1
- pole_admit: float32 [4, 6, 4096], P('net', None, 'line'), may hold values from 0.2 to 0.95
- residue_admit: float32 [4, 6, 3, 3, 4096], P('net', None, None, None, 'line'), may hold values from -1 to 1
- wave_state: float32 [4, 6, 3, 96, 4096], P('net', None, None, None, 'line'), may hold values from -4 to 4
- admit_state: float32 [4, 6, 3, 96, 4096], P('net', None, None, None, 'line'), may hold values from -4 to 4
- wave_history: float32 [4, 4, 3, 96, 4096], P('net', None, None, None, 'line'), may hold values from -6 to 6
Outputs:
- final_voltage: float32 [4, 96, 4096], P('net', None, 'line')
- end_current: float32 [4, 3, 96, 4096], P('net', None, None, 'line')
Inputs may be any that keep to these rules, and one draw needn't show every extreme that they name: `conductance_inverse`: each block is exactly symmetric. `ownership`: A slot is live exactly when the slot of the same number j % 512 at its partner owner is live; the number of live slots differs from owner to owner. The far end of slot j lies in the slot of the same number j % 512 at the partner owner, the partner of that slot is the first owner again, never the owner itself, and at most 17 live slots of one owner have the same partner; this many occur. `delay_steps`: equal at both ends of a line.
All inputs are finite; a program needn't handle non-finite values.
Results may differ from a plain program's by a relative error of at most 0.0003.
Values sent between devices are 32-bit elements; how exact they have to be, the bound alone decides.
A program may use at most 128 MiB of HBM per device.

v0:
```python
import functools

import jax
import jax.numpy as jnp
from jax import lax
from jax.experimental import pallas as pl
from jax.experimental.pallas import tpu as pltpu
from jax.sharding import PartitionSpec as P

STEPS = 3
CORES = 2
MESH = pl.DeviceIdType.MESH


def mix_residue(residue, vector):
    return (
        residue[:, :, 0, None, :] * vector[0]
        + residue[:, :, 1, None, :] * vector[1]
        + residue[:, :, 2, None, :] * vector[2]
    )


def select_delayed(buffer, delay_local):
    depth_count = buffer.shape[0]
    chosen = delay_local[None, :] == jnp.arange(1, depth_count + 1, dtype=jnp.int32)[:, None]
    return jnp.sum(jnp.where(chosen[:, None, None, :], buffer, 0.0), axis=0)


def split_two(value):
    high = value.astype(jnp.bfloat16)
    low = (value - high.astype(jnp.float32)).astype(jnp.bfloat16)
    return high, low


def dot_nt(left, right):
    return lax.dot_general(left, right, (((1,), (1,)), ((), ())), preferred_element_type=jnp.float32)


def dot_nn(left, right):
    return lax.dot_general(left, right, (((1,), (0,)), ((), ())), preferred_element_type=jnp.float32)


def positions(chips):
    line = lax.axis_index("line")
    return line, line // CORES, line % CORES


def greet(chips):
    line, z, core = positions(chips)
    barrier = pltpu.get_barrier_semaphore()
    pl.semaphore_signal(barrier, inc=1, device_id={"line": z * CORES + 1 - core}, device_id_type=MESH)
    for i in range(chips - 1):
        peer = lax.rem(z + 1 + i, chips) * CORES + core
        pl.semaphore_signal(barrier, inc=1, device_id={"line": peer}, device_id_type=MESH)
    pl.semaphore_wait(barrier, chips)


def remote(src, dst, send, recv, line_index):
    return pltpu.make_async_remote_copy(
        src_ref=src, dst_ref=dst, send_sem=send, recv_sem=recv,
        device_id={"line": line_index}, device_id_type=MESH,
    )


def gather_blocks(chips, buf, sems, consume):
    c_send, c_recv, d_send, d_recv = sems
    line, z, core = positions(chips)
    partner = z * CORES + 1 - core

    def across(i):
        peer = lax.rem(z + 1 + i, chips) * CORES + core
        return remote(buf.at[line], buf.at[line], c_send.at[i], c_recv.at[i], peer)

    def over(i, block):
        return remote(buf.at[block], buf.at[block], d_send.at[i], d_recv.at[i], partner)

    for i in range(chips - 1):
        across(i).start()

    def step(k, carry):
        i = lax.rem(k + chips - 1, chips)
        source = lax.rem(z + 2 * chips - 1 - i, chips)
        block = source * CORES + core

        @pl.when(k > 0)
        def _():
            remote(buf.at[block], buf.at[block], c_send.at[i], c_recv.at[i], partner).wait_recv()

        over(i, block).start()
        consume(block)
        other = source * CORES + 1 - core
        remote(buf.at[other], buf.at[other], d_send.at[i], d_recv.at[i], partner).wait_recv()
        consume(other)
        return carry

    lax.fori_loop(0, chips, step, 0)
    for i in range(chips - 1):
        across(i).wait_send()
    for i in range(chips):
        source = lax.rem(z + 2 * chips - 1 - i, chips)
        over(i, source * CORES + core).wait_send()


def one_hot(term_ref, phase, block, width):
    slots = term_ref.shape[1]
    rows = lax.broadcasted_iota(jnp.int32, (width, slots), 0) + block * width
    return (rows == term_ref[phase : phase + 1, :]).astype(jnp.float32).astype(jnp.bfloat16)


def pick_terminals(chips, buf, sems, term_ref, ends_ref):
    phases, count, _ = ends_ref.shape
    width = buf.shape[2]
    ends_ref[...] = jnp.zeros_like(ends_ref)

    def consume(block):
        both = jnp.concatenate(split_two(buf[block]), axis=0)
        for p in range(phases):
            got = dot_nn(both, one_hot(term_ref, p, block, width))
            ends_ref[p] += got[:count] + got[count:]

    gather_blocks(chips, buf, sems, consume)


def prior_kernel(chips, prior_ref, term_ref, ends_ref, vfull, *sems):
    line, z, core = positions(chips)
    greet(chips)
    vfull[line] = prior_ref[...]
    pick_terminals(chips, vfull, sems, term_ref, ends_ref)


def step_kernel(
    chips, h_ref, term_ref, add_ref, inv_hbm, volt_ref, ends_ref,
    part, r1, summed, r2, ifull, vfull, inv, inv_sem,
    a_send, a_recv, b_send, b_recv, *sems,
):
    line, z, core = positions(chips)
    partner = z * CORES + 1 - core
    phases = h_ref.shape[0]
    count, width = add_ref.shape
    load = pltpu.make_async_copy(inv_hbm, inv, inv_sem)
    load.start()
    greet(chips)

    def scatter_block(block):
        total = jnp.zeros((count, width), jnp.float32)
        for p in range(phases):
            both = jnp.concatenate(split_two(h_ref[p]), axis=0)
            got = dot_nt(both, one_hot(term_ref, p, block, width))
            total = total + (got[:count] + got[count:])
        return total

    def swap(i):
        return remote(part.at[i], r1.at[i], a_send.at[i], a_recv.at[i], partner)

    def pass_on(i):
        peer = lax.rem(z + 1 + i, chips) * CORES + core
        return remote(summed.at[i], r2.at[i], b_send.at[i], b_recv.at[i], peer)

    def scatter_step(i, carry):
        target = lax.rem(z + 1 + i, chips)
        part[i] = scatter_block(target * CORES + 1 - core)
        swap(i).start()
        own = scatter_block(target * CORES + core)
        swap(i).wait_recv()
        summed[i] = own + r1[i]

        @pl.when(i < chips - 1)
        def _():
            pass_on(i).start()

        return carry

    lax.fori_loop(0, chips, scatter_step, 0)
    total = summed[chips - 1] + add_ref[...]
    for i in range(chips - 1):
        pass_on(i).wait_recv()
        total = total + r2[i]
    ifull[line] = total
    load.wait()
    volt_ref[...] = jnp.zeros_like(volt_ref)

    def solve(block):
        both = jnp.concatenate(split_two(ifull[block]), axis=0)
        start = pl.multiple_of(block * width, width)
        high, low = split_two(inv[:, pl.ds(start, width)])
        got = dot_nt(both, high)
        volt_ref[...] += got[:count] + (got[count:] + dot_nt(both[:count], low))

    gather_blocks(chips, ifull, sems[:4], solve)
    vfull[line] = volt_ref[...]
    pick_terminals(chips, vfull, sems[4:], term_ref, ends_ref)
    for i in range(chips):
        swap(i).wait_send()
    for i in range(chips - 1):
        pass_on(i).wait_send()


def gather_sems(chips):
    return [
        pltpu.SemaphoreType.DMA((chips,)),
        pltpu.SemaphoreType.DMA((chips,)),
        pltpu.SemaphoreType.DMA((chips,)),
        pltpu.SemaphoreType.DMA((chips,)),
    ]


def vmem():
    return pl.BlockSpec(memory_space=pltpu.VMEM)


def prior_ends(prior, terminal, lines):
    chips = lines // CORES
    count, width = prior.shape
    return pl.pallas_call(
        functools.partial(prior_kernel, chips),
        out_shape=jax.ShapeDtypeStruct((terminal.shape[0], count, terminal.shape[1]), jnp.float32),
        in_specs=[vmem(), vmem()],
        out_specs=vmem(),
        scratch_shapes=[pltpu.VMEM((lines, count, width), jnp.float32)] + gather_sems(chips),
        compiler_params=pltpu.CompilerParams(collective_id=1, has_side_effects=True),
        name="prior_ends",
    )(prior, terminal)


def network_step(h, terminal, extra, inverse, lines):
    chips = lines // CORES
    count, width = extra.shape
    block = lambda n: pltpu.VMEM((n, count, width), jnp.float32)
    return pl.pallas_call(
        functools.partial(step_kernel, chips),
        out_shape=(
            jax.ShapeDtypeStruct((count, width), jnp.float32),
            jax.ShapeDtypeStruct(h.shape, jnp.float32),
        ),
        in_specs=[vmem(), vmem(), vmem(), pl.BlockSpec(memory_space=pltpu.HBM)],
        out_specs=(vmem(), vmem()),
        scratch_shapes=[
            block(chips), block(chips), block(chips), block(chips), block(lines), block(lines),
            pltpu.VMEM(inverse.shape, jnp.float32),
            pltpu.SemaphoreType.DMA(()),
        ] + gather_sems(chips) + gather_sems(chips) + gather_sems(chips),
        compiler_params=pltpu.CompilerParams(
            collective_id=0, has_side_effects=True, vmem_limit_bytes=40 * 2**20
        ),
        name="network_step",
    )(h, terminal, extra, inverse)


def on_device(
    conductance_inverse,
    prior_voltage,
    sources,
    fault_node,
    fault_conductance,
    terminal_node,
    ownership,
    partner,
    delay_steps,
    surge_conductance,
    pole_wave,
    residue_wave,
    pole_admit,
    residue_admit,
    wave_state,
    admit_state,
    wave_history,
):
    inverse_block = conductance_inverse[0]
    row_count = inverse_block.shape[0]
    node_count = inverse_block.shape[1]
    line_index = lax.axis_index("line")
    net_index = lax.axis_index("net")
    line_count = lax.axis_size("line")
    devices = lax.axis_size("net") * line_count
    slot_count = ownership.shape[1]
    capacity = (slot_count + devices - 2) // (devices - 1)
    is_live = ownership[0] > 0
    live_float = is_live.astype(jnp.float32)
    terminal = terminal_node[0]
    delay_local = delay_steps[0]
    surge_local = surge_conductance[0]
    partners = partner[0]
    slot_range = jnp.arange(slot_count, dtype=jnp.int32)
    earlier = (
        (partners[:, None] == partners[None, :])
        & is_live[:, None]
        & (slot_range[:, None] < slot_range[None, :])
    )
    slot_rank = jnp.sum(earlier.astype(jnp.int32), axis=0)
    position = jnp.where(is_live, partners * capacity + slot_rank, devices * capacity)
    place = jnp.arange(devices * capacity, dtype=jnp.int32)
    packer = (place[:, None] == position[None, :]).astype(jnp.float32)
    fault_local = fault_node - (net_index * node_count + line_index * row_count)
    fault_hit = fault_local[:, None] == jnp.arange(row_count, dtype=jnp.int32)[None, :]
    fault_weight = jnp.where(fault_hit, fault_conductance[:, None], 0.0)
    wave_decay = pole_wave[0][:, None, None, :]
    admit_decay = pole_admit[0][:, None, None, :]
    wave_res = residue_wave[0]
    admit_res = residue_admit[0]
    voltage_rows = prior_voltage[0]
    wave_now = wave_state[0]
    admits = admit_state[0]
    history_buffer = wave_history[0]
    ends = prior_ends(voltage_rows, terminal, line_count)
    outgoing = None
    current = None
    for step_index in range(STEPS):
        if step_index == 0:
            wave_now = wave_decay * wave_now + mix_residue(
                wave_res, select_delayed(history_buffer, delay_local)
            )
            admits = admit_decay * admits + mix_residue(admit_res, ends)
        else:
            rows = outgoing.reshape(-1, slot_count)
            buffer = lax.dot_general(
                packer, rows, (((1,), (1,)), ((), ())), precision=lax.Precision.HIGHEST
            )
            arrived = lax.all_to_all(
                buffer, ("net", "line"), split_axis=0, concat_axis=0, tiled=True
            )
            admits = admit_decay * admits + mix_residue(admit_res, ends)
            arrived = lax.dot_general(
                arrived, packer, (((0,), (0,)), ((), ())), precision=lax.Precision.HIGHEST
            ).reshape(outgoing.shape)
            history_buffer = jnp.concatenate([arrived[None], history_buffer[:-1]], axis=0)
            wave_now = wave_decay * wave_now + mix_residue(
                wave_res, select_delayed(history_buffer, delay_local)
            )
        history = (jnp.sum(wave_now, axis=0) - jnp.sum(admits, axis=0)) * live_float
        extra = sources[step_index, 0][None, :] - fault_weight * voltage_rows
        voltage_rows, ends = network_step(history, terminal, extra, inverse_block, line_count)
        if step_index + 1 < STEPS:
            outgoing = (2.0 * surge_local * ends - history) * live_float
        else:
            current = (surge_local * ends - history) * live_float
    return (voltage_rows[None], current[None])


def solution(mesh):
    return jax.shard_map(
        on_device,
        mesh=mesh,
        in_specs=(
            P("net", "line", None),
            P("net", None, "line"),
            P(None, "net", "line"),
            P(),
            P(),
            P("net", None, "line"),
            P("net", "line"),
            P("net", "line"),
            P("net", "line"),
            P("net", "line"),
            P("net", None, "line"),
            P("net", None, None, None, "line"),
            P("net", None, "line"),
            P("net", None, None, None, "line"),
            P("net", None, None, None, "line"),
            P("net", None, None, None, "line"),
            P("net", None, None, None, "line"),
        ),
        out_specs=(P("net", None, "line"), P("net", None, None, "line")),
        check_vma=False,
    )
```

profile of v0, /device:TPU:1, one launch (start us, length us, event | category | flops | bytes accessed | tf_op | source)
XLA Modules:
  0.0 332.9 jit_solution(16209524137777095615)
XLA Ops:
  0.7 0.8 broadcast_compare_fusion.1
  1.6 2.1 fusion.5
  3.9 0.6 copy.66
  4.5 23.7 %prior_ends.1 = f32[3,96,512]{2,1,0:T(8,128)} custom-call(f32[96,512]{1,0:T(8,128)} %bitcast.147, s32[3,512]{1,0:T(4,128)} %bitcast.132), custom_call_target="tpu_custom_call" | custom-call | tf_op jit(solution)/shard_map/prior_ends/pallas_call | solution.py:214
  28.2 1.2 slice_bitcast_fusion.18
  29.7 0.6 fusion.26
  30.3 0.2 convert_reduce_fusion
  30.7 3.1 fusion.22
  33.9 3.2 fusion.23
  37.2 0.1 subtract_multiply_fusion.4.h_ref
  37.3 0.1 fusion.19.add_ref
  37.4 3.4 %copy-done = f32[1,512,4096]{2,1,0:T(8,128)S(1)} copy-done((f32[1,512,4096]{2,1,0:T(8,128)S(1)}, f32[1,512,4096]{2,1,0:T(8,128)}, u32[]{:S(2)}) %copy-start) | copy-done | bytes 8388632
  40.8 65.7 %network_step.3 = (f32[96,512]{1,0:T(8,128)S(1)}, f32[3,96,512]{2,1,0:T(8,128)S(1)}) custom-call(f32[3,96,512]{2,1,0:T(8,128)S(1)} %subtract_multiply_fusion.4.h_ref, s32[3,512]{1,0:T(4,128)S(1)} %bitcast.133, f32[96,512]{1,0:T(8,128)S(1)} %fusion.19.add_ref, f32[512,4096]{1,0:T(8,128)S(1)} %bitcast.127), custom_call_target="tpu_custom_call" | custom-call | tf_op jit(solution)/shard_map/network_step/pallas_call | solution.py:229
  106.5 0.1 subtract_multiply_fusion.3
  106.7 0.2 broadcast_compare_fusion
  106.9 2.6 fusion.11
  109.5 7.0 %all-to-all-start = ((f32[32,17,288]{2,1,0:T(8,128)}), f32[32,17,288]{2,1,0:T(8,128)S(1)}, u32[]{:S(2)}, u32[]{:S(2)}) async-start(f32[32,17,288]{2,1,0:T(8,128)} %fusion.11), calls=%async_computation | async-start | bytes 2359296 | tf_op jit(solution)/shard_map/all_to_all | solution.py:318
  116.6 0.1 fusion.20.add_ref
  116.8 2.1 slice_bitcast_fusion
  118.9 0.3 copy-done.3
  119.4 2.6 fusion.7
  122.0 24.3 %all-to-all-done = f32[32,17,288]{2,1,0:T(8,128)S(1)} async-done(((f32[32,17,288]{2,1,0:T(8,128)}), f32[32,17,288]{2,1,0:T(8,128)S(1)}, u32[]{:S(2)}, u32[]{:S(2)}) %all-to-all-start) | async-done | bytes 626720 | tf_op jit(solution)/shard_map/all_to_all | solution.py:318
  146.3 1.0 all_to_all.13
  147.3 1.4 copy.28
  148.8 1.6 convolution_bitcast_fusion.1
  150.5 1.5 fusion.8
  151.9 0.3 fusion.3
  152.4 0.7 copy-done.4
  153.1 1.8 fusion.6
  154.9 0.1 subtract_multiply_fusion.2.h_ref
  155.0 1.2 slice-done.1
  156.2 63.0 %network_step.4 = (f32[96,512]{1,0:T(8,128)S(1)}, f32[3,96,512]{2,1,0:T(8,128)S(1)}) custom-call(f32[3,96,512]{2,1,0:T(8,128)S(1)} %subtract_multiply_fusion.2.h_ref, s32[3,512]{1,0:T(4,128)S(1)} %bitcast.134, f32[96,512]{1,0:T(8,128)S(1)} %fusion.20.add_ref, f32[512,4096]{1,0:T(8,128)S(1)} %bitcast.130), custom_call_target="tpu_custom_call" | custom-call | tf_op jit(solution)/shard_map/network_step/pallas_call | solution.py:229
  219.3 0.1 subtract_multiply_fusion.1
  219.4 2.5 fusion.9
  221.9 5.4 %all-to-all-start.1 = ((f32[32,17,288]{2,1,0:T(8,128)}), f32[32,17,288]{2,1,0:T(8,128)S(1)}, u32[]{:S(2)}, u32[]{:S(2)}) async-start(f32[32,17,288]{2,1,0:T(8,128)} %fusion.9), calls=%async_computation.1 | async-start | bytes 2359296 | tf_op jit(solution)/shard_map/all_to_all | solution.py:318
  227.4 0.8 fusion.21.add_ref
  228.3 5.1 %add_reduce_fusion = f32[3,96,512]{2,1,0:T(8,128)} fusion(f32[96,512]{1,0:T(8,128)S(1)} %get-tuple-element.15, f32[96,512]{1,0:T(8,128)S(1)} %get-tuple-element.16, f32[96,512]{1,0:T(8,128)S(1)} %get-tuple-element.14, f32[96,512]{1,0:T(8,128)S(1)} %copy-done.30, f32[96,512]{1,0:T(8,128)} %copy-done.31, f32[96,512]{1,0:T(8,128)S(1)} %copy-done.28, ...), kind=kLoop, calls=%fused_computation.4 | loop fusion | flops 19316736 | bytes 6021120 | tf_op jit(solution)/shard_map/reduce_sum | solution.py:329
  233.4 23.7 %all-to-all-done.1 = f32[32,17,288]{2,1,0:T(8,128)S(1)} async-done(((f32[32,17,288]{2,1,0:T(8,128)}), f32[32,17,288]{2,1,0:T(8,128)S(1)}, u32[]{:S(2)}, u32[]{:S(2)}) %all-to-all-start.1) | async-done | bytes 626720 | tf_op jit(solution)/shard_map/all_to_all | solution.py:318
  257.2 1.0 all_to_all.15
  258.2 1.5 copy.30
  259.7 1.8 convolution_bitcast_fusion
  261.5 0.3 fusion.4
  262.0 2.7 add_reduce_fusion.1
  264.7 0.1 subtract_multiply_fusion.h_ref
  264.9 3.4 %copy-done.1 = f32[1,512,4096]{2,1,0:T(8,128)S(1)} copy-done((f32[1,512,4096]{2,1,0:T(8,128)S(1)}, f32[1,512,4096]{2,1,0:T(8,128)}, u32[]{:S(2)}) %copy-start.1) | copy-done | bytes 8388632
  268.2 63.0 %network_step.5 = (f32[96,512]{1,0:T(8,128)S(1)}, f32[3,96,512]{2,1,0:T(8,128)S(1)}) custom-call(f32[3,96,512]{2,1,0:T(8,128)S(1)} %subtract_multiply_fusion.h_ref, s32[3,512]{1,0:T(4,128)S(1)} %bitcast.135, f32[96,512]{1,0:T(8,128)S(1)} %fusion.21.add_ref, f32[512,4096]{1,0:T(8,128)S(1)} %bitcast.131), custom_call_target="tpu_custom_call" | custom-call | tf_op jit(solution)/shard_map/network_step/pallas_call | solution.py:229
  331.3 0.9 multiply_bitcast_fusion
  332.2 0.7 copy.69
  (170 shorter events, 1.0 us)
Async XLA Ops:
  0.7 3.2 copy-start.67
  0.7 28.7 %copy-start.56 = (f32[1,6,3,3,512]{4,0,3,2,1:T(1,128)S(1)}, f32[1,6,3,3,512]{4,0,3,2,1:T(1,128)}, u32[]{:S(2)}) copy-start(f32[1,6,3,3,512]{4,0,3,2,1:T(1,128)} %param.30) | copy-start | bytes 331780
  1.5 28.0 %copy-start.62 = (f32[1,6,512]{2,0,1:T(1,128)S(1)}, f32[1,6,512]{2,0,1:T(1,128)}, u32[]{:S(2)}) copy-start(f32[1,6,512]{2,0,1:T(1,128)} %param.29) | copy-start | bytes 36868
  1.5 28.1 %copy-start.66 = (s32[1,512]{1,0:T(1,128)S(1)}, s32[1,512]{1,0:T(1,128)}, u32[]{:S(2)}) copy-start(s32[1,512]{1,0:T(1,128)} %param.23) | copy-start | bytes 6148
  1.5 28.1 %copy-start.68 = (f32[3,1,512]{2,1,0:T(1,128)S(1)}, f32[3,1,512]{2,1,0:T(1,128)}, u32[]{:S(2)}) copy-start(f32[3,1,512]{2,1,0:T(1,128)} %param.19) | copy-start | bytes 18436
  1.5 28.7 %copy-start.63 = (f32[1,512]{1,0:T(1,128)S(1)}, f32[1,512]{1,0:T(1,128)}, u32[]{:S(2)}) copy-start(f32[1,512]{1,0:T(1,128)} %param.26) | copy-start | bytes 6148
  1.5 28.7 %copy-start.60 = (s32[1,512]{1,0:T(1,128)S(1)}, s32[1,512]{1,0:T(1,128)}, u32[]{:S(2)}) copy-start(s32[1,512]{1,0:T(1,128)} %param.24) | copy-start | bytes 6148
  1.6 29.1 %copy-start.73 = (s32[96]{0:T(128)S(1)}, s32[96]{0:T(128)}, u32[]{:S(2)}) copy-start(s32[96]{0:T(128)} %param.20) | copy-start | bytes 1156
  3.7 27.0 %copy-start.7 = (f32[96,512]{1,0:T(8,128)}, f32[96,512]{1,0:T(8,128)S(1)}, u32[]{:S(2)}) copy-start(f32[96,512]{1,0:T(8,128)S(1)} %get-tuple-element.31) | copy-start | bytes 589828
  3.9 30.0 %copy-start.32 = (f32[6,3,1,512]{3,1,2,0:T(4,128)}, f32[6,3,1,512]{3,1,2,0:T(4,128)S(1)}, u32[]{:S(2)}) copy-start(f32[6,3,1,512]{3,1,2,0:T(4,128)S(1)} %copy.63) | copy-start | bytes 110596
  3.9 29.9 %copy-start.50 = (f32[1,6,512]{2,1,0:T(8,128)}, f32[1,6,512]{2,1,0:T(8,128)S(1)}, u32[]{:S(2)}) copy-start(f32[1,6,512]{2,1,0:T(8,128)S(1)} %copy.65) | copy-start | bytes 36868
  29.4 7.7 %copy-start.10 = (f32[96,512]{1,0:T(8,128)}, f32[96,512]{1,0:T(8,128)S(1)}, u32[]{:S(2)}) copy-start(f32[96,512]{1,0:T(8,128)S(1)} %get-tuple-element.26) | copy-start | bytes 589828
  29.4 7.7 %copy-start.13 = (f32[96,512]{1,0:T(8,128)}, f32[96,512]{1,0:T(8,128)S(1)}, u32[]{:S(2)}) copy-start(f32[96,512]{1,0:T(8,128)S(1)} %get-tuple-element.27) | copy-start | bytes 589828
  29.4 7.7 %copy-start.16 = (f32[96,512]{1,0:T(8,128)}, f32[96,512]{1,0:T(8,128)S(1)}, u32[]{:S(2)}) copy-start(f32[96,512]{1,0:T(8,128)S(1)} %get-tuple-element.28) | copy-start | bytes 589828
  29.6 7.5 %copy-start.41 = (f32[6,3,1,512]{3,1,2,0:T(4,128)}, f32[6,3,1,512]{3,1,2,0:T(4,128)S(1)}, u32[]{:S(2)}) copy-start(f32[6,3,1,512]{3,1,2,0:T(4,128)S(1)} %copy.62) | copy-start | bytes 110596
  29.6 7.5 %copy-start.53 = (f32[1,6,512]{2,1,0:T(8,128)}, f32[1,6,512]{2,1,0:T(8,128)S(1)}, u32[]{:S(2)}) copy-start(f32[1,6,512]{2,1,0:T(8,128)S(1)} %copy.64) | copy-start | bytes 36868
  30.3 76.3 %copy-start.58 = (f32[512]{0:T(512)}, f32[512]{0:T(512)S(1)}, u32[]{:S(2)}) copy-start(f32[512]{0:T(512)S(1)} %broadcast_multiply_fusion) | copy-start | bytes 6148
  30.5 76.2 %copy-start.57 = (s32[1,512]{1,0:T(1,128)}, s32[1,512]{1,0:T(1,128)S(1)}, u32[]{:S(2)}) copy-start(s32[1,512]{1,0:T(1,128)S(1)} %compare_select_fusion) | copy-start | bytes 6148
  30.6 3.3 copy-start.35
  30.6 3.3 copy-start.38
  30.6 6.5 %copy-start.43 = (f32[6,3,512]{2,1,0:T(4,128)}, f32[6,3,512]{2,1,0:T(4,128)S(1)}, u32[]{:S(2)}) copy-start(f32[6,3,512]{2,1,0:T(4,128)S(1)} %get-tuple-element.43) | copy-start | bytes 110596
  30.6 6.5 %copy-start.45 = (f32[6,3,512]{2,1,0:T(4,128)}, f32[6,3,512]{2,1,0:T(4,128)S(1)}, u32[]{:S(2)}) copy-start(f32[6,3,512]{2,1,0:T(4,128)S(1)} %get-tuple-element.44) | copy-start | bytes 110596
  30.7 6.6 %copy-start.71 = (s32[96]{0:T(128)}, s32[96]{0:T(128)S(1)}, u32[]{:S(2)}) copy-start(s32[96]{0:T(128)S(1)} %broadcast_subtract_fusion) | copy-start | bytes 1156
  33.8 3.4 %copy-start.47 = (f32[1,96,512]{2,1,0:T(8,128)S(1)}, f32[1,96,512]{2,1,0:T(8,128)}, u32[]{:S(2)}) copy-start(f32[1,96,512]{2,1,0:T(8,128)} %param.18) | copy-start | bytes 589828
  33.9 3.4 %copy-start.69 = (f32[96]{0:T(128)S(1)}, f32[96]{0:T(128)}, u32[]{:S(2)}) copy-start(f32[96]{0:T(128)} %param.21) | copy-start | bytes 1156
  33.9 3.5 %copy-start.2 = (s32[1,3,512]{2,1,0:T(4,128)S(1)}, s32[1,3,512]{2,1,0:T(4,128)}, u32[]{:S(2)}) copy-start(s32[1,3,512]{2,1,0:T(4,128)} %copy.66) | copy-start | bytes 18436
  37.4 3.4 %copy-start = (f32[1,512,4096]{2,1,0:T(8,128)S(1)}, f32[1,512,4096]{2,1,0:T(8,128)}, u32[]{:S(2)}) copy-start(f32[1,512,4096]{2,1,0:T(8,128)} %param.17) | copy-start | bytes 25165828
  106.5 10.1 %copy-start.65 = (f32[1,1,512]{2,1,0:T(1,128)S(1)}, f32[1,1,512]{2,1,0:T(1,128)}, u32[]{:S(2)}) copy-start(f32[1,1,512]{2,1,0:T(1,128)} %get-tuple-element.40) | copy-start | bytes 6148
  106.5 10.1 %copy-start.70 = (f32[96]{0:T(128)S(1)}, f32[96]{0:T(128)}, u32[]{:S(2)}) copy-start(f32[96]{0:T(128)} %param.21) | copy-start | bytes 1156
  106.5 10.1 %copy-start.72 = (s32[96]{0:T(128)S(1)}, s32[96]{0:T(128)}, u32[]{:S(2)}) copy-start(s32[96]{0:T(128)} %copy-done.71) | copy-start | bytes 1156
  106.9 9.8 %copy-start.48 = (pred[32,17,512]{2,0,1:T(32,128)(4,1)}, pred[32,17,512]{2,0,1:T(32,128)(4,1)S(1)}, u32[]{:S(2)}) copy-start(pred[32,17,512]{2,0,1:T(32,128)(4,1)S(1)} %broadcast_compare_fusion) | copy-start | bytes 835588
  109.5 36.8 %all-to-all-start = ((f32[32,17,288]{2,1,0:T(8,128)}), f32[32,17,288]{2,1,0:T(8,128)S(1)}, u32[]{:S(2)}, u32[]{:S(2)}) async-start(f32[32,17,288]{2,1,0:T(8,128)} %fusion.11), calls=%async_computation | async-start | bytes 2359296 | tf_op jit(solution)/shard_map/all_to_all | solution.py:318
  150.5 4.6 %slice-start = ((s8[8388608]{0:T(1024)(128)(4,1)}), s8[4194304]{0:T(1024)(128)(4,1)S(1)}, s32[]{:S(2)}) async-start(s8[8388608]{0:T(1024)(128)(4,1)} %bitcast.128), calls=%async_computation.2 | async-start | bytes 8388608
  152.3 3.9 %slice-start.1 = ((s8[8388608]{0:T(1024)(128)(4,1)}), s8[4194304]{0:T(1024)(128)(4,1)S(1)}, s32[]{:S(2)}) async-start(s8[8388608]{0:T(1024)(128)(4,1)} %bitcast.128), calls=%async_computation.3 | async-start | bytes 8388608
  156.2 63.0 %copy-start.59 = (f32[512]{0:T(512)S(1)}, f32[512]{0:T(512)}, u32[]{:S(2)}) copy-start(f32[512]{0:T(512)} %copy-done.58) | copy-start | bytes 6148
  156.2 63.2 %copy-start.49 = (pred[32,17,512]{2,0,1:T(32,128)(4,1)S(1)}, pred[32,17,512]{2,0,1:T(32,128)(4,1)}, u32[]{:S(2)}) copy-start(pred[32,17,512]{2,0,1:T(32,128)(4,1)} %copy-done.48) | copy-start | bytes 835588
  219.4 8.9 %copy-start.12 = (f32[96,512]{1,0:T(8,128)S(1)}, f32[96,512]{1,0:T(8,128)}, u32[]{:S(2)}) copy-start(f32[96,512]{1,0:T(8,128)} %copy-done.10) | copy-start | bytes 589828
  219.4 8.9 %copy-start.15 = (f32[96,512]{1,0:T(8,128)S(1)}, f32[96,512]{1,0:T(8,128)}, u32[]{:S(2)}) copy-start(f32[96,512]{1,0:T(8,128)} %copy-done.13) | copy-start | bytes 589828
  219.4 8.9 %copy-start.18 = (f32[96,512]{1,0:T(8,128)S(1)}, f32[96,512]{1,0:T(8,128)}, u32[]{:S(2)}) copy-start(f32[96,512]{1,0:T(8,128)} %copy-done.16) | copy-start | bytes 589828
  219.4 8.9 %copy-start.28 = (f32[96,512]{1,0:T(8,128)S(1)}, f32[96,512]{1,0:T(8,128)}, u32[]{:S(2)}) copy-start(f32[96,512]{1,0:T(8,128)} %copy-done.27) | copy-start | bytes 589828
  219.4 8.9 %copy-start.30 = (f32[96,512]{1,0:T(8,128)S(1)}, f32[96,512]{1,0:T(8,128)}, u32[]{:S(2)}) copy-start(f32[96,512]{1,0:T(8,128)} %copy-done.29) | copy-start | bytes 589828
  221.9 35.2 %all-to-all-start.1 = ((f32[32,17,288]{2,1,0:T(8,128)}), f32[32,17,288]{2,1,0:T(8,128)S(1)}, u32[]{:S(2)}, u32[]{:S(2)}) async-start(f32[32,17,288]{2,1,0:T(8,128)} %fusion.9), calls=%async_computation.1 | async-start | bytes 2359296 | tf_op jit(solution)/shard_map/all_to_all | solution.py:318
  233.4 28.1 %copy-start.6 = (f32[3,3,96,512]{3,2,1,0:T(8,128)S(1)}, f32[3,3,96,512]{3,2,1,0:T(8,128)}, u32[]{:S(2)}) copy-start(f32[3,3,96,512]{3,2,1,0:T(8,128)} %fusion.8) | copy-start | bytes 5308420
  258.2 3.7 %copy-start.9 = (f32[96,512]{1,0:T(8,128)S(1)}, f32[96,512]{1,0:T(8,128)}, u32[]{:S(2)}) copy-start(f32[96,512]{1,0:T(8,128)} %copy-done.7) | copy-start | bytes 589828
  258.2 3.7 %copy-start.22 = (f32[96,512]{1,0:T(8,128)S(1)}, f32[96,512]{1,0:T(8,128)}, u32[]{:S(2)}) copy-start(f32[96,512]{1,0:T(8,128)} %copy-done.21) | copy-start | bytes 589828
  258.2 3.7 %copy-start.34 = (f32[6,3,1,512]{3,1,2,0:T(4,128)S(1)}, f32[6,3,1,512]{3,1,2,0:T(4,128)}, u32[]{:S(2)}) copy-start(f32[6,3,1,512]{3,1,2,0:T(4,128)} %copy-done.32) | copy-start | bytes 110596
  264.9 3.4 %copy-start.1 = (f32[1,512,4096]{2,1,0:T(8,128)S(1)}, f32[1,512,4096]{2,1,0:T(8,128)}, u32[]{:S(2)}) copy-start(f32[1,512,4096]{2,1,0:T(8,128)} %param.17) | copy-start | bytes 25165828
  268.2 63.0 %copy-start.64 = (f32[1,512]{1,0:T(1,128)S(1)}, f32[1,512]{1,0:T(1,128)}, u32[]{:S(2)}) copy-start(f32[1,512]{1,0:T(1,128)} %param.26) | copy-start | bytes 6148
  (30 other events, 77.5 us)
where the time goes:
time: 334 us; the launch traced here: 333 us
  Pallas kernels  215 us (64%)
  waiting for transfers between devices  48 us (14%)
  other arithmetic  26.6 us (8%)
  local copies, waits for them, and re-layouts  20 us (6%)
  starting transfers between devices  12.5 us (4%)
  matrix products  8.42 us (3%)
    pallas_call x3, Pallas kernels, network_step(): pl.pallas_call(functools.partial(step_kernel, chips), out_shape=(jax.Shap...  192 us
    all_to_all x2, waiting for transfers between devices, on_device(): lax.all_to_all(buffer, ('net', 'line'), split_axis=0, concat_axis=0, tile...  48 us
    pallas_call x1, Pallas kernels, prior_ends(): pl.pallas_call(functools.partial(prior_kernel, chips), out_shape=jax.Shap...  23.7 us
    reduce_sum x6, other arithmetic, on_device(): history = (jnp.sum(wave_now, axis=0) - jnp.sum(admits, axis=0)) * live_float  18.6 us
    all_to_all x2, starting transfers between devices, on_device(): lax.all_to_all(buffer, ('net', 'line'), split_axis=0, concat_axis=0, tile...  12.5 us
    unnamed x162, local copies, waits for them, and re-layouts  10.8 us
  transfers between devices with their start and end apart: 2, of which 2 were waited for; matrix products, arithmetic and copies ran while one was open for 3% of the time, Pallas kernels for 0%

commit v1 on v0

v1 whole, which is shorter than its diff:
```python
import functools

import jax
import jax.numpy as jnp
from jax import lax
from jax.experimental import pallas as pl
from jax.experimental.pallas import tpu as pltpu
from jax.sharding import PartitionSpec as P

STEPS = 3
CORES = 2
SPLIT = 2
LANES = 128
SUBLANES = 8
MESH = pl.DeviceIdType.MESH


def split_two(value):
    high = value.astype(jnp.bfloat16)
    low = (value - high.astype(jnp.float32)).astype(jnp.bfloat16)
    return high, low


def stack_two(value):
    return jnp.concatenate(split_two(value), axis=0)


def fold_two(value):
    half = value.shape[0] // 2
    return value[:half] + value[half:]


def dot_nt(left, right):
    return lax.dot_general(left, right, (((1,), (1,)), ((), ())), preferred_element_type=jnp.float32)


def dot_nn(left, right):
    return lax.dot_general(left, right, (((1,), (0,)), ((), ())), preferred_element_type=jnp.float32)


def as_hot(mask):
    return mask.astype(jnp.float32).astype(jnp.bfloat16)


def message_plan(capacity, width):
    tiles, rest = width // LANES, width % LANES
    groups = LANES // rest
    base = capacity // SUBLANES * SUBLANES
    spare = (capacity - base) * tiles
    left = -(-(spare + -(-capacity // groups)) // SUBLANES) * SUBLANES
    return tiles, rest, groups, base, spare, left


def kernel(
    lines, nets,
    prior_ref, source_ref, fnode_ref, fcond_ref, term_ref, live_ref, partner_ref, delay_ref, surge_ref,
    polew_ref, resw_ref, polea_ref, resa_ref, inv_hbm, wave_hbm, admit_hbm, hist_hbm,
    volt_ref, curr_ref,
    inv, wave, admit, hist, inv_high, inv_low, hot, pack_main, pack_left, left_rhs,
    coef_w, coef_a, hist_sum, ends, h, h_split, fault, ifull, vfull,
    part, r1, mine, rbuf, xsend, xrecv,
    load_sem, a_send, a_recv, b_send, b_recv,
    ic_send, ic_recv, id_send, id_recv, vc_send, vc_recv, vd_send, vd_recv, x_send, x_recv,
):
    chips = lines // CORES
    devices = lines * nets
    net = lax.axis_index("net")
    line = lax.axis_index("line")
    z = line // CORES
    core = lax.rem(line, CORES)
    me = net * lines + line
    mate = z * CORES + 1 - core
    phases, count, slots = h.shape
    width = ifull.shape[2]
    nodes = width * lines
    half = count // SPLIT
    capacity = (slots + devices - 2) // (devices - 1)
    tiles, rest, groups, base, spare, left = message_plan(capacity, phases * count)
    lead = tiles * base

    def remote(src, dst, send, recv, target):
        return pltpu.make_async_remote_copy(
            src_ref=src, dst_ref=dst, send_sem=send, recv_sem=recv,
            device_id={"line": target}, device_id_type=MESH,
        )

    def nearest(e):
        near = jnp.minimum(z, chips - 1 - z)
        both = jnp.where(lax.rem(e, 2) == 1, z - (e + 1) // 2, z + e // 2)
        one = jnp.where(z > near, z - (e - near), z + (e - near))
        return jnp.where(e <= 2 * near, both, one)

    def rows(s):
        return pl.ds(s * half, half)

    loads = [
        pltpu.make_async_copy(src, dst, load_sem.at[i])
        for i, (src, dst) in enumerate(
            ((wave_hbm, wave), (admit_hbm, admit), (hist_hbm, hist), (inv_hbm, inv))
        )
    ]
    for load in loads:
        load.start()

    barrier = pltpu.get_barrier_semaphore()

    def greet(i, carry):
        peer = lax.rem(me + 1 + i, devices)
        pl.semaphore_signal(
            barrier, inc=1, device_id={"net": peer // lines, "line": lax.rem(peer, lines)},
            device_id_type=MESH,
        )
        return carry

    lax.fori_loop(0, devices - 1, greet, 0)
    vfull[line] = prior_ref[...]
    ends[...] = jnp.zeros_like(ends)
    xrecv[:, me] = jnp.zeros_like(xrecv[:, me])
    left_rhs[...] = jnp.zeros_like(left_rhs)
    pl.semaphore_wait(barrier, devices - 1)

    def gather_start(buf, sems):
        c_send, c_recv, d_send, d_recv = sems
        for s in range(SPLIT):
            view = buf.at[line, rows(s)]

            @pl.when(z + 1 < chips)
            def _():
                remote(view, view, c_send.at[0, z, s], c_recv.at[z, s], line + CORES).start()

            @pl.when(z > 0)
            def _():
                remote(view, view, c_send.at[1, z, s], c_recv.at[z, s], line - CORES).start()

            remote(view, view, d_send.at[z, s], d_recv.at[z, s], mate).start()

    def gather(buf, sems, consume, fill=None):
        c_send, c_recv, d_send, d_recv = sems

        def step(e, carry):
            source = nearest(e)
            block = source * CORES + core
            other = source * CORES + 1 - core

            @pl.when(e > 0)
            def _():
                for s in range(SPLIT):
                    view = buf.at[block, rows(s)]
                    remote(view, view, c_send.at[0, source, s], c_recv.at[source, s], mate).wait_recv()

                    @pl.when((source < z) & (z + 1 < chips))
                    def _():
                        remote(view, view, c_send.at[0, source, s], c_recv.at[source, s], line + CORES).start()

                    @pl.when((source > z) & (z > 0))
                    def _():
                        remote(view, view, c_send.at[1, source, s], c_recv.at[source, s], line - CORES).start()

                    remote(view, view, d_send.at[source, s], d_recv.at[source, s], mate).start()

            if fill is not None:
                fill(e)

            def take(j, carry):
                @pl.when(j == 1)
                def _():
                    for s in range(SPLIT):
                        view = buf.at[other, rows(s)]
                        remote(view, view, d_send.at[source, s], d_recv.at[source, s], mate).wait_recv()

                consume(source * CORES + lax.rem(core + j, CORES))
                return carry

            lax.fori_loop(0, CORES, take, 0)
            return carry

        lax.fori_loop(0, chips, step, 0)

        def drain(source, carry):
            block = source * CORES + core
            for s in range(SPLIT):
                view = buf.at[block, rows(s)]
                remote(view, view, d_send.at[source, s], d_recv.at[source, s], mate).wait_send()

                @pl.when((source <= z) & (z + 1 < chips))
                def _():
                    remote(view, view, c_send.at[0, source, s], c_recv.at[source, s], mate).wait_send()

                @pl.when((source >= z) & (z > 0))
                def _():
                    remote(view, view, c_send.at[1, source, s], c_recv.at[source, s], mate).wait_send()

            return carry

        lax.fori_loop(0, chips, drain, 0)

    def pick(block):
        both = stack_two(vfull[block])
        for p in range(phases):
            ends[p] += fold_two(dot_nn(both, hot[p, block]))

    def spread(block):
        total = jnp.zeros((count, width), jnp.float32)
        for p in range(phases):
            total = total + fold_two(dot_nt(h_split[p], hot[p, block]))
        return total

    def solve(block):
        both = stack_two(ifull[block])
        got = dot_nt(both, inv_high[block])
        volt_ref[...] += got[:count] + (got[count:] + dot_nt(both[:count], inv_low[block]))

    def build_hot():
        def one(block, carry):
            lane = lax.broadcasted_iota(jnp.int32, (width, slots), 0) + block * width
            for p in range(phases):
                hot[p, block] = as_hot(lane == term_ref[p : p + 1, :])
            return carry

        lax.fori_loop(0, lines, one, 0)

    def build_inverse():
        loads[3].wait()

        def one(block, carry):
            high, low = split_two(inv[:, pl.ds(pl.multiple_of(block * width, width), width)])
            inv_high[block] = high
            inv_low[block] = low
            return carry

        lax.fori_loop(0, lines, one, 0)

    def build_coef():
        poles = polew_ref.shape[0]
        for pole_ref, res_ref, coef in ((polew_ref, resw_ref, coef_w), (polea_ref, resa_ref, coef_a)):
            for p in range(phases):
                for r in range(phases):
                    power = [res_ref[q, p, r : r + 1, :] for q in range(poles)]
                    for m in range(STEPS):
                        total = power[0]
                        for q in range(1, poles):
                            total = total + power[q]
                        coef[m, p * phases + r : p * phases + r + 1, :] = total
                        if m + 1 < STEPS:
                            power = [power[q] * pole_ref[q : q + 1, :] for q in range(poles)]

    def build_history():
        for load in loads[:3]:
            load.wait()
        poles = polew_ref.shape[0]
        depth = hist.shape[0]
        delay = delay_ref[...]
        groups_of_rows = count // SUBLANES

        def one(g, carry):
            at = pl.ds(pl.multiple_of(g * SUBLANES, SUBLANES), SUBLANES)
            old = []
            for t in range(1, STEPS + 1):
                per_phase = []
                for r in range(phases):
                    value = jnp.zeros((SUBLANES, slots), jnp.float32)
                    for d in range(t, depth + 1):
                        value = jnp.where(delay == d, hist[d - t, r, at, :], value)
                    per_phase.append(value)
                old.append(per_phase)
            for p in range(phases):
                sums = [jnp.zeros((SUBLANES, slots), jnp.float32) for _ in range(STEPS)]
                for q in range(poles):
                    x = wave[q, p, at, :]
                    y = admit[q, p, at, :]
                    for t in range(STEPS):
                        x = x * polew_ref[q : q + 1, :]
                        y = y * polea_ref[q : q + 1, :]
                        sums[t] = sums[t] + (x - y)
                for t in range(STEPS):
                    for s in range(t + 1):
                        for r in range(phases):
                            row = p * phases + r
                            sums[t] = sums[t] + coef_w[t - s, row : row + 1, :] * old[s][r]
                    hist_sum[t, p, at, :] = sums[t]
            return carry

        lax.fori_loop(0, groups_of_rows, one, 0)

    def build_packers():
        owner = lax.broadcasted_iota(jnp.int32, (devices, slots), 0)
        hits = as_hot((owner == partner_ref[...]) & (live_ref[...] > 0))
        before = as_hot(
            lax.broadcasted_iota(jnp.int32, (slots, slots), 0)
            < lax.broadcasted_iota(jnp.int32, (slots, slots), 1)
        )
        counts = dot_nn(hits, before) * hits.astype(jnp.float32)
        rank = jnp.sum(counts, axis=0, keepdims=True).astype(jnp.int32)
        stride = slots
        place = jnp.where(live_ref[...] > 0, partner_ref[...] * stride + rank, -1)
        if base:
            row = lax.broadcasted_iota(jnp.int32, (devices * base, slots), 0)
            pack_main[...] = as_hot((row // base) * stride + lax.rem(row, base) == place)
        row = lax.broadcasted_iota(jnp.int32, (devices * left, slots), 0)
        owner = row // left
        index = lax.rem(row, left)
        for k in range(groups + tiles):
            if k < groups:
                wanted = (index - spare) * groups + k
                fits = (index >= spare) & (wanted < capacity)
            else:
                wanted = base + index // tiles
                fits = (index < spare) & (lax.rem(index, tiles) == k - groups)
            wanted = jnp.where(fits, owner * stride + wanted, -2)
            pack_left[:, k * slots : (k + 1) * slots] = as_hot(wanted == place)

    def build_fault():
        local = fnode_ref[...] - (net * nodes + line * width)
        lane = lax.broadcasted_iota(jnp.int32, (count, width), 1)
        fault[...] = jnp.where(lane == local, fcond_ref[...], 0.0)

    def fill_prior(e):
        @pl.when(e == 0)
        def _():
            build_hot()

        @pl.when(e == 1)
        def _():
            build_coef()
            build_fault()

        @pl.when(e == 2)
        def _():
            build_inverse()

        @pl.when(e == chips - 1)
        def _():
            build_history()
            build_packers()

    def scatter_sum():
        def finish(e):
            target = nearest(chips - 1 - e)
            remote(part.at[target], r1.at[target], a_send.at[target], a_recv.at[target], mate).wait_recv()
            mine[target] = mine[target] + r1[target]
            pass_on(target, (z == 0) & (target > z), (z == chips - 1) & (target < z))

        def pass_on(target, right, left_way):
            for s in range(SPLIT):
                pass_half(target, s, right, left_way)

        def pass_half(target, s, right, left_way):
            @pl.when(right)
            def _():
                remote(
                    mine.at[target, rows(s)], rbuf.at[0, target, rows(s)],
                    b_send.at[target, s], b_recv.at[0, target, s], line + CORES,
                ).start()

            @pl.when(left_way)
            def _():
                remote(
                    mine.at[target, rows(s)], rbuf.at[1, target, rows(s)],
                    b_send.at[target, s], b_recv.at[1, target, s], line - CORES,
                ).start()

        def compute(e, carry):
            target = nearest(chips - 1 - e)

            def both(j, carry):
                got = spread(target * CORES + lax.rem(core + 1 + j, CORES))

                @pl.when(j == 0)
                def _():
                    part[target] = got
                    remote(
                        part.at[target], r1.at[target], a_send.at[target], a_recv.at[target], mate
                    ).start()

                @pl.when(j == 1)
                def _():
                    mine[target] = got

                return carry

            lax.fori_loop(0, CORES, both, 0)

            @pl.when(e > 0)
            def _():
                finish(e - 1)

            return carry

        lax.fori_loop(0, chips, compute, 0)
        finish(chips - 1)

        def arrive(side, target, s):
            remote(
                mine.at[target, rows(s)], rbuf.at[side, target, rows(s)],
                b_send.at[target, s], b_recv.at[side, target, s], mate,
            ).wait_recv()
            mine[target, rows(s)] = mine[target, rows(s)] + rbuf[side, target, rows(s)]

        def relay(e, carry):
            target = nearest(chips - 1 - e)
            for s in range(SPLIT):
                @pl.when((target >= z) & (z > 0))
                def _():
                    arrive(0, target, s)

                @pl.when((target <= z) & (z + 1 < chips))
                def _():
                    arrive(1, target, s)

                pass_half(target, s, (target > z) & (z > 0), (target < z) & (z + 1 < chips))
            return carry

        lax.fori_loop(0, chips, relay, 0)

    def scatter_drain():
        def one(target, carry):
            remote(part.at[target], r1.at[target], a_send.at[target], a_recv.at[target], mate).wait_send()

            @pl.when(target < z)
            def _():
                for s in range(SPLIT):
                    remote(
                        mine.at[target, rows(s)], rbuf.at[0, target, rows(s)],
                        b_send.at[target, s], b_recv.at[0, target, s], mate,
                    ).wait_send()

            @pl.when(target > z)
            def _():
                for s in range(SPLIT):
                    remote(
                        mine.at[target, rows(s)], rbuf.at[0, target, rows(s)],
                        b_send.at[target, s], b_recv.at[0, target, s], mate,
                    ).wait_send()

            return carry

        lax.fori_loop(0, chips, one, 0)

    def exchange_copy(t, i):
        peer = lax.rem(me + 1 + i, devices)
        return pltpu.make_async_remote_copy(
            src_ref=xsend.at[peer], dst_ref=xrecv.at[t, me], send_sem=x_send.at[i],
            recv_sem=x_recv.at[t, i],
            device_id={"net": peer // lines, "line": lax.rem(peer, lines)}, device_id_type=MESH,
        )

    def exchange_start(t):
        surge = surge_ref[...]
        live = live_ref[...].astype(jnp.float32)
        wave_out = jnp.concatenate(
            [(2.0 * surge * ends[p] - h[p]) * live for p in range(phases)], axis=0
        )
        high, low = split_two(wave_out)
        body = tiles * LANES
        if base:
            main = dot_nt(pack_main[...], jnp.concatenate([high[:body], low[:body]], axis=0))
            main = main[:, :body] + main[:, body:]
            for j in range(tiles):
                xsend[:, j * base : (j + 1) * base, :] = main[:, j * LANES : (j + 1) * LANES].reshape(
                    devices, base, LANES
                )
        for offset, value in ((0, high), (LANES, low)):
            for k in range(groups):
                left_rhs[offset + k * rest : offset + (k + 1) * rest, k * slots : (k + 1) * slots] = value[body:]
            for j in range(tiles):
                left_rhs[offset : offset + LANES, (groups + j) * slots : (groups + j + 1) * slots] = value[
                    j * LANES : (j + 1) * LANES
                ]
        tail = dot_nt(pack_left[...], left_rhs[...])
        tail = tail[:, :LANES] + tail[:, LANES:]
        xsend[:, lead : lead + left, :] = tail.reshape(devices, left, LANES)

        def go(i, carry):
            exchange_copy(t, i).start()
            return carry

        lax.fori_loop(0, devices - 1, go, 0)

    def exchange_finish(t):
        def end(i, carry):
            exchange_copy(t, i).wait()
            return carry

        lax.fori_loop(0, devices - 1, end, 0)

    def unpack(t):
        tail = xrecv[t, :, lead : lead + left, :].reshape(devices * left, LANES).T
        high, low = split_two(tail)
        arrived = []
        if base:
            for j in range(tiles):
                main = xrecv[t, :, j * base : (j + 1) * base, :].reshape(devices * base, LANES).T
                arrived.append(fold_two(dot_nn(stack_two(main), pack_main[...])))
        for j in range(tiles):
            k = groups + j
            more = fold_two(
                dot_nn(jnp.concatenate([high, low], axis=0), pack_left[:, k * slots : (k + 1) * slots])
            )
            if base:
                arrived[j] = arrived[j] + more
            else:
                arrived.append(more)
        last = jnp.zeros((rest, slots), jnp.float32)
        for k in range(groups):
            here = slice(k * rest, (k + 1) * rest)
            last = last + fold_two(
                dot_nn(jnp.concatenate([high[here], low[here]], axis=0), pack_left[:, k * slots : (k + 1) * slots])
            )
        return jnp.concatenate(arrived + [last], axis=0)

    def mixed(coef, m, p, values):
        total = coef[m, p * phases : p * phases + 1, :] * values[0]
        for r in range(1, phases):
            total = total + coef[m, p * phases + r : p * phases + r + 1, :] * values[r]
        return total

    def add_ends(t):
        values = [ends[r] for r in range(phases)]
        for m in range(STEPS):
            @pl.when(t + m < STEPS)
            def _():
                for p in range(phases):
                    hist_sum[t + m, p] = hist_sum[t + m, p] - mixed(coef_a, m, p, values)

    def add_waves(t):
        arrived = unpack(t - 1)
        delay = delay_ref[...]
        for d in range(1, STEPS):
            values = [
                jnp.where(delay == d, arrived[r * count : (r + 1) * count], 0.0) for r in range(phases)
            ]
            for m in range(STEPS - d):
                @pl.when(t + d - 1 + m < STEPS)
                def _():
                    for p in range(phases):
                        at = t + d - 1 + m
                        hist_sum[at, p] = hist_sum[at, p] + mixed(coef_w, m, p, values)

    isems = (ic_send, ic_recv, id_send, id_recv)
    vsems = (vc_send, vc_recv, vd_send, vd_recv)
    gather_start(vfull, vsems)
    gather(vfull, vsems, pick, fill_prior)

    def run_step(t, carry):
        add_ends(t)

        @pl.when(t > 0)
        def _():
            exchange_finish(t - 1)
            add_waves(t)

        live = live_ref[...].astype(jnp.float32)
        for p in range(phases):
            now = hist_sum[t, p] * live
            h[p] = now
            h_split[p] = stack_two(now)
        extra = source_ref[t] - fault[...] * vfull[line]
        scatter_sum()
        ifull[line] = mine[z] + extra
        gather_start(ifull, isems)
        volt_ref[...] = jnp.zeros_like(volt_ref)
        gather(ifull, isems, solve)
        vfull[line] = volt_ref[...]
        gather_start(vfull, vsems)
        scatter_drain()
        ends[...] = jnp.zeros_like(ends)
        gather(vfull, vsems, pick)

        @pl.when(t + 1 < STEPS)
        def _():
            exchange_start(t)

        return carry

    lax.fori_loop(0, STEPS, run_step, 0)
    live = live_ref[...].astype(jnp.float32)
    for p in range(phases):
        curr_ref[p] = (surge_ref[...] * ends[p] - h[p]) * live


def on_device(
    conductance_inverse, prior_voltage, sources, fault_node, fault_conductance, terminal_node,
    ownership, partner, delay_steps, surge_conductance, pole_wave, residue_wave, pole_admit,
    residue_admit, wave_state, admit_state, wave_history,
):
    lines = lax.axis_size("line")
    nets = lax.axis_size("net")
    devices = lines * nets
    chips = lines // CORES
    inverse = conductance_inverse[0]
    prior = prior_voltage[0]
    terminal = terminal_node[0]
    count, width = prior.shape
    phases, slots = terminal.shape
    wave = wave_state[0]
    admit = admit_state[0]
    hist = wave_history[0]
    capacity = (slots + devices - 2) // (devices - 1)
    tiles, rest, groups, base, spare, left = message_plan(capacity, phases * count)
    message = tiles * base + left
    f32, bf16 = jnp.float32, jnp.bfloat16
    vmem = lambda: pl.BlockSpec(memory_space=pltpu.VMEM)
    hbm = lambda: pl.BlockSpec(memory_space=pltpu.HBM)
    dma = lambda *shape: pltpu.SemaphoreType.DMA(shape)
    gather_sems = [
        dma(2, chips, SPLIT), dma(chips, SPLIT), dma(chips, SPLIT), dma(chips, SPLIT),
    ]
    volt, curr = pl.pallas_call(
        functools.partial(kernel, lines, nets),
        out_shape=(
            jax.ShapeDtypeStruct((count, width), f32),
            jax.ShapeDtypeStruct((phases, count, slots), f32),
        ),
        in_specs=[vmem()] * 13 + [hbm()] * 4,
        out_specs=(vmem(), vmem()),
        scratch_shapes=[
            pltpu.VMEM(inverse.shape, f32),
            pltpu.VMEM(wave.shape, f32),
            pltpu.VMEM(admit.shape, f32),
            pltpu.VMEM(hist.shape, f32),
            pltpu.VMEM((lines, inverse.shape[0], width), bf16),
            pltpu.VMEM((lines, inverse.shape[0], width), bf16),
            pltpu.VMEM((phases, lines, width, slots), bf16),
            pltpu.VMEM((devices * max(base, SUBLANES), slots), bf16),
            pltpu.VMEM((devices * left, (groups + tiles) * slots), bf16),
            pltpu.VMEM((2 * LANES, (groups + tiles) * slots), bf16),
            pltpu.VMEM((STEPS, phases * phases, slots), f32),
            pltpu.VMEM((STEPS, phases * phases, slots), f32),
            pltpu.VMEM((STEPS, phases, count, slots), f32),
            pltpu.VMEM((phases, count, slots), f32),
            pltpu.VMEM((phases, count, slots), f32),
            pltpu.VMEM((phases, 2 * count, slots), bf16),
            pltpu.VMEM((count, width), f32),
            pltpu.VMEM((lines, count, width), f32),
            pltpu.VMEM((lines, count, width), f32),
            pltpu.VMEM((chips, count, width), f32),
            pltpu.VMEM((chips, count, width), f32),
            pltpu.VMEM((chips, count, width), f32),
            pltpu.VMEM((2, chips, count, width), f32),
            pltpu.VMEM((devices, message, LANES), f32),
            pltpu.VMEM((STEPS - 1, devices, message, LANES), f32),
            dma(4), dma(chips), dma(chips), dma(chips, SPLIT), dma(2, chips, SPLIT),
        ] + gather_sems + gather_sems + [dma(devices), dma(STEPS - 1, devices)],
        compiler_params=pltpu.CompilerParams(
            collective_id=0, has_side_effects=True, vmem_limit_bytes=67043328
        ),
        name="network",
    )(
        prior, sources, fault_node[:, None], fault_conductance[:, None], terminal, ownership, partner,
        delay_steps, surge_conductance, pole_wave[0], residue_wave[0], pole_admit[0], residue_admit[0],
        inverse, wave, admit, hist,
    )
    return volt[None], curr[None]


def solution(mesh):
    return jax.shard_map(
        on_device,
        mesh=mesh,
        in_specs=(
            P("net", "line", None),
            P("net", None, "line"),
            P(None, "net", "line"),
            P(),
            P(),
            P("net", None, "line"),
            P("net", "line"),
            P("net", "line"),
            P("net", "line"),
            P("net", "line"),
            P("net", None, "line"),
            P("net", None, None, None, "line"),
            P("net", None, "line"),
            P("net", None, None, None, "line"),
            P("net", None, None, None, "line"),
            P("net", None, None, None, "line"),
            P("net", None, None, None, "line"),
        ),
        out_specs=(P("net", None, "line"), P("net", None, None, "line")),
        check_vma=False,
    )
```

time: 334 us -> 256 us (0.77)
  waiting for transfers between devices: 48 us -> 0 us
  Pallas kernels: 215 us -> 245 us
  other arithmetic: 26.6 us -> 0 us
  starting transfers between devices: 12.5 us -> 0 us
  local copies, waits for them, and re-layouts: 20 us -> 10.6 us
  matrix products: 8.42 us -> 0 us
    all_to_all x2 -> x0, waiting for transfers between devices: 48 us -> none  [on_device(): lax.all_to_all(buffer, ('net', 'line'), split_axis=0, concat_axis=0, tile...]
    pallas_call x4 -> x1, Pallas kernels: 215 us -> 245 us  [on_device(): pl.pallas_call(functools.partial(kernel, lines, nets), out_shape=(jax.Sha...]
    reduce_sum x10 -> x0, other arithmetic: 21.5 us -> none  [the longest x6 18.6 us: on_device(): history = (jnp.sum(wave_now, axis=0) - jnp.sum(admits, axis=0)) * live_float]
    all_to_all x2 -> x0, starting transfers between devices: 12.5 us -> none  [on_device(): lax.all_to_all(buffer, ('net', 'line'), split_axis=0, concat_axis=0, tile...]
    dot_general x4 -> x0, matrix products: 8.42 us -> none  [the longest x2 5.06 us: on_device(): lax.dot_general(packer, rows, (((1,), (1,)), ((), ())), precision=lax.Pre...]
    unnamed x162 -> x5, local copies, waits for them, and re-layouts: 10.8 us -> 7.9 us
  transfers between devices with their start and end apart: 2 -> 0, of which waited for: 2 -> 0; matrix products, arithmetic and copies ran while one was open for 3% -> 0% of each run, Pallas kernels for 0% -> 0%
where the time goes in v1:
time: 256 us
  Pallas kernels  245 us (96%)
  local copies, waits for them, and re-layouts  10.6 us (4%)
    pallas_call x1, Pallas kernels, on_device(): pl.pallas_call(functools.partial(kernel, lines, nets), out_shape=(jax.Sha...  245 us
    unnamed x5, local copies, waits for them, and re-layouts  7.9 us

profile of v1, /device:TPU:1, one launch (start us, length us, event | category | flops | bytes accessed | tf_op | source)
XLA Modules:
  0.0 256.0 jit_solution(5179507631926043347)
XLA Ops:
  0.6 1.3 copy.31
  1.9 1.3 copy_bitcast_fusion.2
  3.3 1.4 copy.19.fnode_ref
  4.6 1.4 copy.20.fcond_ref
  6.0 1.7 copy_bitcast_fusion
  7.7 244.7 %network.1 = (f32[96,512]{1,0:T(8,128)}, f32[3,96,512]{2,1,0:T(8,128)}) custom-call(f32[96,512]{1,0:T(8,128)} %bitcast.25, f32[3,1,512]{2,1,0:T(1,128)} %source_ref.1, s32[96,1]{1,0:T(8,128)} %copy.19.fnode_ref, f32[96,1]{1,0:T(8,128)} %copy.20.fcond_ref, s32[3,512]{1,0:T(4,128)} %bitcast.27, s32[1,512]{1,0:T(1,128)} %live_ref.1, s32[1,512]{1,0:T(1,128)} %partner_ref.1, ...), custom_call_target="tpu_custom_call" | custom-call | tf_op jit(solution)/shard_map/network/pallas_call | solution.py:608
  252.5 1.6 copy.34
  254.1 1.9 copy.35

commit v2 on v1

v2 whole, which is shorter than its diff:
```python
import functools

import jax
import jax.numpy as jnp
from jax import lax
from jax.experimental import pallas as pl
from jax.experimental.pallas import tpu as pltpu
from jax.sharding import PartitionSpec as P

STEPS = 3
CORES = 2
SPLIT = 2
PIECES = 3
LANES = 128
SUBLANES = 8
MESH = pl.DeviceIdType.MESH


def split_two(value):
    high = value.astype(jnp.bfloat16)
    low = (value - high.astype(jnp.float32)).astype(jnp.bfloat16)
    return high, low


def stack_two(value):
    return jnp.concatenate(split_two(value), axis=0)


def fold_two(value):
    half = value.shape[0] // 2
    return value[:half] + value[half:]


def dot_nt(left, right):
    return lax.dot_general(left, right, (((1,), (1,)), ((), ())), preferred_element_type=jnp.float32)


def dot_nn(left, right):
    return lax.dot_general(left, right, (((1,), (0,)), ((), ())), preferred_element_type=jnp.float32)


def as_hot(mask):
    return mask.astype(jnp.float32).astype(jnp.bfloat16)


def message_plan(capacity, width):
    tiles, rest = width // LANES, width % LANES
    groups = LANES // rest
    base = capacity // SUBLANES * SUBLANES
    spare = (capacity - base) * tiles
    left = -(-(spare + -(-capacity // groups)) // SUBLANES) * SUBLANES
    return tiles, rest, groups, base, spare, left


def kernel(
    lines, nets,
    prior_ref, source_ref, fnode_ref, fcond_ref, term_ref, live_ref, partner_ref, delay_ref, surge_ref,
    polew_ref, resw_ref, polea_ref, resa_ref, inv_hbm, wave_hbm, admit_hbm, hist_hbm,
    volt_ref, curr_ref,
    wave, admit, hist, inv_high, inv_low, hot, hot_t, pack_main, pack_left, left_rhs,
    coef_w, coef_a, hist_sum, ends, h, h_split, fault, ifull, vfull,
    part, r1, mine, rbuf, xsend, xrecv,
    load_sem, inv_sem, a_send, a_recv, b_send, b_recv,
    ic_send, ic_recv, id_send, id_recv, vc_send, vc_recv, vd_send, vd_recv, x_send, x_recv,
):
    chips = lines // CORES
    devices = lines * nets
    net = lax.axis_index("net")
    line = lax.axis_index("line")
    z = line // CORES
    core = lax.rem(line, CORES)
    me = net * lines + line
    mate = z * CORES + 1 - core
    phases, count, slots = h.shape
    width = ifull.shape[2]
    nodes = width * lines
    half = count // SPLIT
    piece = half // PIECES
    poles = polew_ref.shape[0]
    depth = hist.shape[0] // (phases * count)
    capacity = (slots + devices - 2) // (devices - 1)
    tiles, rest, groups, base, spare, left = message_plan(capacity, phases * half)
    lead = tiles * base
    turned = len(hot_t.shape) == 4

    def remote(src, dst, send, recv, target):
        return pltpu.make_async_remote_copy(
            src_ref=src, dst_ref=dst, send_sem=send, recv_sem=recv,
            device_id={"line": target}, device_id_type=MESH,
        )

    def nearest(e):
        near = jnp.minimum(z, chips - 1 - z)
        both = jnp.where(lax.rem(e, 2) == 1, z - (e + 1) // 2, z + e // 2)
        one = jnp.where(z > near, z - (e - near), z + (e - near))
        return jnp.where(e <= 2 * near, both, one)

    def rows(s):
        return pl.ds(pl.multiple_of(s * half, half), half)

    def bits(s, i):
        return pl.ds(pl.multiple_of(s * half + i * piece, piece), piece)

    states = ((wave_hbm, wave), (admit_hbm, admit), (hist_hbm, hist))
    loads = [pltpu.make_async_copy(src, dst, load_sem.at[i]) for i, (src, dst) in enumerate(states)]
    for load in loads:
        load.start()

    places = [(dst, at) for _, dst in states for at in range(0, dst.shape[0] - width + 1, width)][:lines]

    def stage(block):
        dst, at = places[block]
        return pltpu.make_async_copy(
            inv_hbm.at[:, pl.ds(block * width, width)], dst.at[pl.ds(at, width), pl.ds(0, width)],
            inv_sem.at[block],
        )

    barrier = pltpu.get_barrier_semaphore()

    def greet(i, carry):
        peer = lax.rem(me + 1 + i, devices)
        pl.semaphore_signal(
            barrier, inc=1, device_id={"net": peer // lines, "line": lax.rem(peer, lines)},
            device_id_type=MESH,
        )
        return carry

    lax.fori_loop(0, devices - 1, greet, 0)
    vfull[line] = prior_ref[...]
    xrecv[:, :, me] = jnp.zeros_like(xrecv[:, :, me])

    def gather_hop(buf, sems, block, source, s, i, side, to):
        view = buf.at[block, bits(s, i)]
        return remote(view, view, sems[0].at[side, source, s, i], sems[1].at[source, s, i], to)

    def gather_start(buf, sems, s):
        c_send, c_recv, d_send, d_recv = sems

        @pl.when(z + 1 < chips)
        def _():
            for i in range(PIECES):
                gather_hop(buf, sems, line, z, s, i, 0, line + CORES).start()

        @pl.when(z > 0)
        def _():
            for i in range(PIECES):
                gather_hop(buf, sems, line, z, s, i, 1, line - CORES).start()

        view = buf.at[line, rows(s)]
        remote(view, view, d_send.at[z, s], d_recv.at[z, s], mate).start()

    def gather_arrive(buf, sems, s, e):
        c_send, c_recv, d_send, d_recv = sems
        source = nearest(e)
        block = source * CORES + core

        @pl.when(e > 0)
        def _():
            for i in range(PIECES):
                gather_hop(buf, sems, block, source, s, i, 0, mate).wait_recv()

                @pl.when((source < z) & (z + 1 < chips))
                def _():
                    gather_hop(buf, sems, block, source, s, i, 0, line + CORES).start()

                @pl.when((source > z) & (z > 0))
                def _():
                    gather_hop(buf, sems, block, source, s, i, 1, line - CORES).start()

            view = buf.at[block, rows(s)]
            remote(view, view, d_send.at[source, s], d_recv.at[source, s], mate).start()

    def gather_take(buf, sems, s, e, consume):
        c_send, c_recv, d_send, d_recv = sems

        def take(j, carry):
            source = nearest(jnp.maximum(e - j, 0))

            @pl.when((e < chips) & (j == 0))
            def _():
                consume(source * CORES + core, s)

            @pl.when((e > 0) & (j == 1))
            def _():
                view = buf.at[source * CORES + 1 - core, rows(s)]
                remote(view, view, d_send.at[source, s], d_recv.at[source, s], mate).wait_recv()
                consume(source * CORES + 1 - core, s)

            return carry

        lax.fori_loop(0, CORES, take, 0)

    def gather_last(buf, sems, s, consume):
        source = nearest(chips - 1)
        view = buf.at[source * CORES + 1 - core, rows(s)]
        remote(view, view, sems[2].at[source, s], sems[3].at[source, s], mate).wait_recv()
        consume(source * CORES + 1 - core, s)

    def gather_drain(buf, sems, s):
        c_send, c_recv, d_send, d_recv = sems

        def drain(source, carry):
            block = source * CORES + core
            view = buf.at[block, rows(s)]
            remote(view, view, d_send.at[source, s], d_recv.at[source, s], mate).wait_send()

            @pl.when((source <= z) & (z + 1 < chips))
            def _():
                for i in range(PIECES):
                    gather_hop(buf, sems, block, source, s, i, 0, mate).wait_send()

            @pl.when((source >= z) & (z > 0))
            def _():
                for i in range(PIECES):
                    gather_hop(buf, sems, block, source, s, i, 1, mate).wait_send()

            return carry

        lax.fori_loop(0, chips, drain, 0)

    def pick(block, s):
        both = stack_two(vfull[block, rows(s)])
        for p in range(phases):
            ends[p, rows(s)] += fold_two(dot_nn(both, hot[p, block]))

    def spread(block, s):
        total = jnp.zeros((half, width), jnp.float32)
        for p in range(phases):
            if turned:
                total = total + fold_two(dot_nn(h_split[p], hot_t[p, block]))
            else:
                total = total + fold_two(dot_nt(h_split[p], hot[p, block]))
        return total

    def solve(block, s):
        both = stack_two(ifull[block, rows(s)])
        got = dot_nn(both, inv_high[block])
        volt_ref[rows(s)] += got[:half] + (got[half:] + dot_nn(both[:half], inv_low[block]))

    def build_hot():
        def one(block, carry):
            lane = lax.broadcasted_iota(jnp.int32, (width, slots), 0) + block * width
            for p in range(phases):
                hot[p, block] = as_hot(lane == term_ref[p])
            return carry

        lax.fori_loop(0, lines, one, 0)

    def build_hot_t():
        for p in range(phases):
            tall = jnp.broadcast_to(term_ref[p].astype(jnp.float32), (LANES, slots)).T.astype(jnp.int32)
            lane = lax.broadcasted_iota(jnp.int32, (slots, LANES), 1)

            def one(block, carry):
                for j in range(width // LANES):
                    hot_t[p, block, :, j * LANES : (j + 1) * LANES] = as_hot(
                        lane + (block * width + j * LANES) == tall
                    )
                return carry

            lax.fori_loop(0, lines, one, 0)

    def build_inverse():
        for block in range(lines):
            dst, at = places[block]
            stage(block).wait()
            high, low = split_two(dst[pl.ds(at, width), :width].T)
            inv_high[block] = high
            inv_low[block] = low

    def build_coef():
        for pole_ref, res_ref, coef in ((polew_ref, resw_ref, coef_w), (polea_ref, resa_ref, coef_a)):
            for p in range(phases):
                for r in range(phases):
                    power = [res_ref[q, p, r] for q in range(poles)]
                    for m in range(STEPS):
                        total = power[0]
                        for q in range(1, poles):
                            total = total + power[q]
                        coef[m, p * phases + r : p * phases + r + 1, :] = total
                        if m + 1 < STEPS:
                            power = [power[q] * pole_ref[q] for q in range(poles)]

    def build_history():
        for load in loads:
            load.wait()
        delay = delay_ref[...]

        def one(g, carry):
            first = pl.multiple_of(g * SUBLANES, SUBLANES)
            at = pl.ds(first, SUBLANES)

            def row(lead_index):
                return pl.ds(pl.multiple_of(lead_index * count + first, SUBLANES), SUBLANES)

            old = []
            for t in range(1, STEPS + 1):
                per_phase = []
                for r in range(phases):
                    value = jnp.zeros((SUBLANES, slots), jnp.float32)
                    for d in range(t, depth + 1):
                        value = jnp.where(delay == d, hist[row((d - t) * phases + r), :], value)
                    per_phase.append(value)
                old.append(per_phase)
            for p in range(phases):
                sums = [jnp.zeros((SUBLANES, slots), jnp.float32) for _ in range(STEPS)]
                for q in range(poles):
                    x = wave[row(q * phases + p), :]
                    y = admit[row(q * phases + p), :]
                    for t in range(STEPS):
                        x = x * polew_ref[q]
                        y = y * polea_ref[q]
                        sums[t] = sums[t] + (x - y)
                for t in range(STEPS):
                    for s in range(t + 1):
                        for r in range(phases):
                            k = p * phases + r
                            sums[t] = sums[t] + coef_w[t - s, k : k + 1, :] * old[s][r]
                    hist_sum[t, p, at, :] = sums[t]
            return carry

        lax.fori_loop(0, count // SUBLANES, one, 0)

    def build_packers():
        owner = lax.broadcasted_iota(jnp.int32, (devices, slots), 0)
        hits = as_hot((owner == partner_ref[...]) & (live_ref[...] > 0))
        before = as_hot(
            lax.broadcasted_iota(jnp.int32, (slots, slots), 0)
            < lax.broadcasted_iota(jnp.int32, (slots, slots), 1)
        )
        counts = dot_nn(hits, before) * hits.astype(jnp.float32)
        rank = jnp.sum(counts, axis=0, keepdims=True).astype(jnp.int32)
        stride = slots
        place = jnp.where(live_ref[...] > 0, partner_ref[...] * stride + rank, -1)
        if base:
            row = lax.broadcasted_iota(jnp.int32, (devices * base, slots), 0)
            pack_main[...] = as_hot((row // base) * stride + lax.rem(row, base) == place)
        row = lax.broadcasted_iota(jnp.int32, (devices * left, slots), 0)
        owner = row // left
        index = lax.rem(row, left)
        for k in range(groups + tiles):
            if k < groups:
                wanted = (index - spare) * groups + k
                fits = (index >= spare) & (wanted < capacity)
            else:
                wanted = base + index // tiles
                fits = (index < spare) & (lax.rem(index, tiles) == k - groups)
            wanted = jnp.where(fits, owner * stride + wanted, -2)
            pack_left[:, k * slots : (k + 1) * slots] = as_hot(wanted == place)

    def build_fault():
        same = lax.broadcasted_iota(jnp.int32, (count, count), 0) == lax.broadcasted_iota(
            jnp.int32, (count, count), 1
        )
        node = jnp.sum(jnp.where(same, fnode_ref[...].astype(jnp.float32), 0.0), axis=1, keepdims=True)
        strength = jnp.sum(jnp.where(same, fcond_ref[...], 0.0), axis=1, keepdims=True)
        local = node.astype(jnp.int32) - (net * nodes + line * width)
        lane = lax.broadcasted_iota(jnp.int32, (count, width), 1)
        fault[...] = jnp.where(lane == local, strength, 0.0)

    def swap(target, s):
        return remote(
            part.at[target, rows(s)], r1.at[target, rows(s)], a_send.at[target, s], a_recv.at[target, s], mate
        )

    def hop(side, target, s, i, to):
        return remote(
            mine.at[target, bits(s, i)], rbuf.at[side, target, bits(s, i)],
            b_send.at[target, s, i], b_recv.at[side, target, s, i], to,
        )

    def pass_on(target, s, i, right, left_way):
        @pl.when(right)
        def _():
            hop(0, target, s, i, line + CORES).start()

        @pl.when(left_way)
        def _():
            hop(1, target, s, i, line - CORES).start()

    def sum_finish(e, s):
        target = nearest(chips - 1 - e)
        swap(target, s).wait_recv()
        mine[target, rows(s)] = mine[target, rows(s)] + r1[target, rows(s)]
        for i in range(PIECES):
            pass_on(target, s, i, (z == 0) & (target > z), (z == chips - 1) & (target < z))

    def sum_compute(s):
        def one(e, carry):
            target = nearest(chips - 1 - e)

            def both(j, carry):
                got = spread(target * CORES + lax.rem(core + 1 + j, CORES), s)

                @pl.when(j == 0)
                def _():
                    part[target, rows(s)] = got
                    swap(target, s).start()

                @pl.when(j == 1)
                def _():
                    mine[target, rows(s)] = got

                return carry

            lax.fori_loop(0, CORES, both, 0)

            @pl.when(e > 0)
            def _():
                sum_finish(e - 1, s)

            return carry

        lax.fori_loop(0, chips, one, 0)
        sum_finish(chips - 1, s)

    def sum_relay(e, s):
        target = nearest(chips - 1 - e)

        def arrive(side, i):
            hop(side, target, s, i, mate).wait_recv()
            mine[target, bits(s, i)] = mine[target, bits(s, i)] + rbuf[side, target, bits(s, i)]

        for i in range(PIECES):
            @pl.when((target >= z) & (z > 0))
            def _():
                arrive(0, i)

            @pl.when((target <= z) & (z + 1 < chips))
            def _():
                arrive(1, i)

            pass_on(target, s, i, (target > z) & (z > 0), (target < z) & (z + 1 < chips))

    def sum_drain(s):
        def one(target, carry):
            swap(target, s).wait_send()

            @pl.when(target != z)
            def _():
                for i in range(PIECES):
                    hop(0, target, s, i, mate).wait_send()

            return carry

        lax.fori_loop(0, chips, one, 0)

    def exchange_copy(t, s, i):
        peer = lax.rem(me + 1 + i, devices)
        return pltpu.make_async_remote_copy(
            src_ref=xsend.at[s, peer], dst_ref=xrecv.at[t, s, me], send_sem=x_send.at[s, i],
            recv_sem=x_recv.at[t, s, i],
            device_id={"net": peer // lines, "line": lax.rem(peer, lines)}, device_id_type=MESH,
        )

    def exchange_start(t, s):
        surge = surge_ref[...]
        live = live_ref[...].astype(jnp.float32)
        wave_out = jnp.concatenate(
            [(2.0 * surge * ends[p, rows(s)] - h[p, rows(s)]) * live for p in range(phases)], axis=0
        )
        high, low = split_two(wave_out)
        body = tiles * LANES
        if base:
            main = dot_nt(pack_main[...], jnp.concatenate([high[:body], low[:body]], axis=0))
            main = main[:, :body] + main[:, body:]
            for j in range(tiles):
                xsend[s, :, j * base : (j + 1) * base, :] = main[:, j * LANES : (j + 1) * LANES].reshape(
                    devices, base, LANES
                )
        for offset, value in ((0, high), (LANES, low)):
            for k in range(groups):
                left_rhs[offset + k * rest : offset + (k + 1) * rest, k * slots : (k + 1) * slots] = value[body:]
            for j in range(tiles):
                left_rhs[offset : offset + LANES, (groups + j) * slots : (groups + j + 1) * slots] = value[
                    j * LANES : (j + 1) * LANES
                ]
        tail = dot_nt(pack_left[...], left_rhs[...])
        tail = tail[:, :LANES] + tail[:, LANES:]
        xsend[s, :, lead : lead + left, :] = tail.reshape(devices, left, LANES)

        def go(i, carry):
            exchange_copy(t, s, i).start()
            return carry

        lax.fori_loop(0, devices - 1, go, 0)

    def exchange_finish(t, s):
        def end(i, carry):
            exchange_copy(t, s, i).wait()
            return carry

        lax.fori_loop(0, devices - 1, end, 0)

    def unpack(t, s):
        tail = xrecv[t, s, :, lead : lead + left, :].reshape(devices * left, LANES).T
        high, low = split_two(tail)
        arrived = []
        if base:
            for j in range(tiles):
                main = xrecv[t, s, :, j * base : (j + 1) * base, :].reshape(devices * base, LANES).T
                arrived.append(fold_two(dot_nn(stack_two(main), pack_main[...])))
        for j in range(tiles):
            k = groups + j
            more = fold_two(
                dot_nn(jnp.concatenate([high, low], axis=0), pack_left[:, k * slots : (k + 1) * slots])
            )
            if base:
                arrived[j] = arrived[j] + more
            else:
                arrived.append(more)
        last = jnp.zeros((rest, slots), jnp.float32)
        for k in range(groups):
            here = slice(k * rest, (k + 1) * rest)
            last = last + fold_two(
                dot_nn(jnp.concatenate([high[here], low[here]], axis=0), pack_left[:, k * slots : (k + 1) * slots])
            )
        return jnp.concatenate(arrived + [last], axis=0)

    def mixed(coef, m, p, values):
        total = coef[m, p * phases : p * phases + 1, :] * values[0]
        for r in range(1, phases):
            total = total + coef[m, p * phases + r : p * phases + r + 1, :] * values[r]
        return total

    def add_ends(t, s):
        values = [ends[r, rows(s)] for r in range(phases)]
        for m in range(STEPS):
            @pl.when(t + m < STEPS)
            def _():
                for p in range(phases):
                    hist_sum[t + m, p, rows(s)] = hist_sum[t + m, p, rows(s)] - mixed(coef_a, m, p, values)

    def add_waves(t, s):
        arrived = unpack(t - 1, s)
        delay = delay_ref[...]
        for d in range(1, STEPS):
            values = [
                jnp.where(delay == d, arrived[r * half : (r + 1) * half], 0.0) for r in range(phases)
            ]
            for m in range(STEPS - d):
                @pl.when(t + d - 1 + m < STEPS)
                def _():
                    for p in range(phases):
                        at = t + d - 1 + m
                        hist_sum[at, p, rows(s)] = hist_sum[at, p, rows(s)] + mixed(coef_w, m, p, values)

    left_rhs[...] = jnp.zeros_like(left_rhs)
    build_coef()
    build_fault()
    pl.semaphore_wait(barrier, devices - 1)
    isems = (ic_send, ic_recv, id_send, id_recv)
    vsems = (vc_send, vc_recv, vd_send, vd_recv)
    for s in range(SPLIT):
        gather_start(vfull, vsems, s)
    ends[...] = jnp.zeros_like(ends)
    build_hot()

    def first(e, carry):
        gather_arrive(vfull, vsems, 0, e)

        @pl.when(e == 1)
        def _():
            if turned:
                build_hot_t()

        @pl.when(e == 2)
        def _():
            build_history()
            for block in range(lines):
                stage(block).start()

        gather_take(vfull, vsems, 0, e, pick)
        return carry

    lax.fori_loop(0, chips, first, 0)
    gather_last(vfull, vsems, 0, pick)
    gather_drain(vfull, vsems, 0)
    add_ends(0, 0)

    def run_half(k, carry):
        s = lax.rem(k, SPLIT)
        o = 1 - s
        t = k // SPLIT
        done = t + s

        @pl.when(t > 0)
        def _():
            exchange_finish(t - 1, s)
            add_waves(t, s)

        live = live_ref[...].astype(jnp.float32)
        for p in range(phases):
            now = hist_sum[t, p, rows(s)] * live
            h[p, rows(s)] = now
            h_split[p] = stack_two(now)
        sum_compute(s)

        @pl.when(k == 0)
        def _():
            build_inverse()

        @pl.when(k > 0)
        def _():
            ends[:, rows(o)] = jnp.zeros_like(ends[:, rows(o)])

        def merged(e, carry):
            gather_arrive(vfull, vsems, o, e)
            sum_relay(e, s)
            gather_take(vfull, vsems, o, e, pick)
            return carry

        lax.fori_loop(0, chips, merged, 0)
        ifull[line, rows(s)] = mine[z, rows(s)] + (source_ref[t] - fault[rows(s)] * vfull[line, rows(s)])
        gather_start(ifull, isems, s)
        gather_last(vfull, vsems, o, pick)
        gather_drain(vfull, vsems, o)

        @pl.when(k == 0)
        def _():
            build_packers()

        @pl.when((done > 0) & (done < STEPS))
        def _():
            exchange_start(done - 1, o)

        @pl.when(done < STEPS)
        def _():
            add_ends(done, o)

        volt_ref[rows(s)] = jnp.zeros_like(volt_ref[rows(s)])

        def answer(e, carry):
            gather_arrive(ifull, isems, s, e)
            gather_take(ifull, isems, s, e, solve)
            return carry

        lax.fori_loop(0, chips, answer, 0)
        gather_last(ifull, isems, s, solve)
        vfull[line, rows(s)] = volt_ref[rows(s)]
        gather_start(vfull, vsems, s)
        gather_drain(ifull, isems, s)
        sum_drain(s)
        return carry

    lax.fori_loop(0, SPLIT * STEPS, run_half, 0)
    o = SPLIT - 1
    ends[:, rows(o)] = jnp.zeros_like(ends[:, rows(o)])

    def final(e, carry):
        gather_arrive(vfull, vsems, o, e)
        gather_take(vfull, vsems, o, e, pick)
        return carry

    lax.fori_loop(0, chips, final, 0)
    gather_last(vfull, vsems, o, pick)
    live = live_ref[...].astype(jnp.float32)
    for p in range(phases):
        curr_ref[p] = (surge_ref[...] * ends[p] - h[p]) * live
    gather_drain(vfull, vsems, o)


def hand_over(volt_ref, curr_ref, volt_out, curr_out):
    volt_out[...] = volt_ref[...]
    curr_out[...] = curr_ref[...]


def on_device(
    conductance_inverse, prior_voltage, sources, fault_node, fault_conductance, terminal_node,
    ownership, partner, delay_steps, surge_conductance, pole_wave, residue_wave, pole_admit,
    residue_admit, wave_state, admit_state, wave_history,
):
    lines = lax.axis_size("line")
    nets = lax.axis_size("net")
    devices = lines * nets
    chips = lines // CORES
    inverse = conductance_inverse[0]
    prior = prior_voltage[0]
    terminal = terminal_node[0]
    count, width = prior.shape
    phases, slots = terminal.shape
    wave = wave_state.reshape(-1, slots)
    admit = admit_state.reshape(-1, slots)
    hist = wave_history.reshape(-1, slots)
    capacity = (slots + devices - 2) // (devices - 1)
    half = count // SPLIT
    tiles, rest, groups, base, spare, left = message_plan(capacity, phases * half)
    message = tiles * base + left
    turned = devices * left <= slots
    f32, bf16 = jnp.float32, jnp.bfloat16
    vmem = lambda: pl.BlockSpec(memory_space=pltpu.VMEM)
    hbm = lambda: pl.BlockSpec(memory_space=pltpu.HBM)
    dma = lambda *shape: pltpu.SemaphoreType.DMA(shape)
    gather_sems = [
        dma(2, chips, SPLIT, PIECES), dma(chips, SPLIT, PIECES), dma(chips, SPLIT), dma(chips, SPLIT),
    ]
    volt, curr = pl.pallas_call(
        functools.partial(kernel, lines, nets),
        out_shape=(
            jax.ShapeDtypeStruct((count, width), f32),
            jax.ShapeDtypeStruct((phases, count, slots), f32),
        ),
        in_specs=[vmem()] * 13 + [hbm()] * 4,
        out_specs=(vmem(), vmem()),
        scratch_shapes=[
            pltpu.VMEM(wave.shape, f32),
            pltpu.VMEM(admit.shape, f32),
            pltpu.VMEM(hist.shape, f32),
            pltpu.VMEM((lines, inverse.shape[0], width), bf16),
            pltpu.VMEM((lines, inverse.shape[0], width), bf16),
            pltpu.VMEM((phases, lines, width, slots), bf16),
            pltpu.VMEM((phases, lines, slots, width) if turned else (SUBLANES, LANES), bf16),
            pltpu.VMEM((devices * max(base, SUBLANES), slots), bf16),
            pltpu.VMEM((devices * left, (groups + tiles) * slots), bf16),
            pltpu.VMEM((2 * LANES, (groups + tiles) * slots), bf16),
            pltpu.VMEM((STEPS, phases * phases, slots), f32),
            pltpu.VMEM((STEPS, phases * phases, slots), f32),
            pltpu.VMEM((STEPS, phases, count, slots), f32),
            pltpu.VMEM((phases, count, slots), f32),
            pltpu.VMEM((phases, count, slots), f32),
            pltpu.VMEM((phases, 2 * half, slots), bf16),
            pltpu.VMEM((count, width), f32),
            pltpu.VMEM((lines, count, width), f32),
            pltpu.VMEM((lines, count, width), f32),
            pltpu.VMEM((chips, count, width), f32),
            pltpu.VMEM((chips, count, width), f32),
            pltpu.VMEM((chips, count, width), f32),
            pltpu.VMEM((2, chips, count, width), f32),
            pltpu.VMEM((SPLIT, devices, message, LANES), f32),
            pltpu.VMEM((STEPS - 1, SPLIT, devices, message, LANES), f32),
            dma(3), dma(lines), dma(chips, SPLIT), dma(chips, SPLIT), dma(chips, SPLIT, PIECES), dma(2, chips, SPLIT, PIECES),
        ] + gather_sems + gather_sems + [dma(SPLIT, devices), dma(STEPS - 1, SPLIT, devices)],
        compiler_params=pltpu.CompilerParams(
            collective_id=0, has_side_effects=True, vmem_limit_bytes=67043328
        ),
        name="network",
    )(
        prior, sources, fault_node[None], fault_conductance[None], terminal[:, None], ownership, partner,
        delay_steps, surge_conductance, pole_wave[0][:, None], residue_wave[0][:, :, :, None],
        pole_admit[0][:, None], residue_admit[0][:, :, :, None],
        inverse, wave, admit, hist,
    )
    volt, curr = pl.pallas_call(
        hand_over,
        out_shape=(jax.ShapeDtypeStruct(volt.shape, f32), jax.ShapeDtypeStruct(curr.shape, f32)),
        in_specs=[vmem(), vmem()],
        out_specs=(vmem(), vmem()),
        name="hand_over",
    )(volt, curr)
    return volt[None], curr[None]


def solution(mesh):
    return jax.shard_map(
        on_device,
        mesh=mesh,
        in_specs=(
            P("net", "line", None),
            P("net", None, "line"),
            P(None, "net", "line"),
            P(),
            P(),
            P("net", None, "line"),
            P("net", "line"),
            P("net", "line"),
            P("net", "line"),
            P("net", "line"),
            P("net", None, "line"),
            P("net", None, None, None, "line"),
            P("net", None, "line"),
            P("net", None, None, None, "line"),
            P("net", None, None, None, "line"),
            P("net", None, None, None, "line"),
            P("net", None, None, None, "line"),
        ),
        out_specs=(P("net", None, "line"), P("net", None, None, "line")),
        check_vma=False,
    )
```

time: 256 us -> 244 us (0.953)
  local copies, waits for them, and re-layouts: 10.6 us -> 0 us
    unnamed x5 -> x0, local copies, waits for them, and re-layouts: 7.9 us -> none
    pallas_call x1, Pallas kernels: 245 us -> 241 us  [on_device(): pl.pallas_call(functools.partial(kernel, lines, nets), out_shape=(jax.Sha...]
    broadcast_in_dim x2 -> x0, local copies, waits for them, and re-layouts: 2.74 us -> none  [the longest x1 1.37 us: on_device(): fault_conductance[:, None]]
where the time goes in v2:
time: 244 us; the launch traced here: 243 us
  Pallas kernels  243 us (100%)
    pallas_call x1, Pallas kernels, on_device(): pl.pallas_call(functools.partial(kernel, lines, nets), out_shape=(jax.Sha...  241 us

profile of v2, /device:TPU:1, one launch (start us, length us, event | category | flops | bytes accessed | tf_op | source)
XLA Modules:
  0.0 243.4 jit_solution(287499949503319657)
XLA Ops:
  0.6 240.7 %network.1 = (f32[96,512]{1,0:T(8,128)}, f32[3,96,512]{2,1,0:T(8,128)}) custom-call(f32[96,512]{1,0:T(8,128)} %bitcast.18, f32[3,1,512]{2,1,0:T(1,128)} %source_ref.1, s32[1,96]{1,0:T(1,128)} %bitcast.24, f32[1,96]{1,0:T(1,128)} %bitcast.25, s32[3,1,512]{2,1,0:T(1,128)} %bitcast.23, s32[1,512]{1,0:T(1,128)} %live_ref.1, s32[1,512]{1,0:T(1,128)} %partner_ref.1, ...), custom_call_target="tpu_custom_call" | custom-call | tf_op jit(solution)/shard_map/network/pallas_call | solution.py:697
  241.3 2.1 hand_over.1

commit v3 on v2

--- a/solution.py
+++ b/solution.py
@@ -82,6 +82,7 @@
     tiles, rest, groups, base, spare, left = message_plan(capacity, phases * half)
     lead = tiles * base
     turned = len(hot_t.shape) == 4
+    used = lead + spare + -(-capacity // groups)
 
     def remote(src, dst, send, recv, target):
         return pltpu.make_async_remote_copy(
@@ -115,6 +116,7 @@
             inv_sem.at[block],
         )
 
+    xrecv[...] = jnp.zeros_like(xrecv)
     barrier = pltpu.get_barrier_semaphore()
 
     def greet(i, carry):
@@ -127,7 +129,6 @@
 
     lax.fori_loop(0, devices - 1, greet, 0)
     vfull[line] = prior_ref[...]
-    xrecv[:, :, me] = jnp.zeros_like(xrecv[:, :, me])
 
     def gather_hop(buf, sems, block, source, s, i, side, to):
         view = buf.at[block, bits(s, i)]
@@ -448,7 +449,7 @@
     def exchange_copy(t, s, i):
         peer = lax.rem(me + 1 + i, devices)
         return pltpu.make_async_remote_copy(
-            src_ref=xsend.at[s, peer], dst_ref=xrecv.at[t, s, me], send_sem=x_send.at[s, i],
+            src_ref=xsend.at[s, peer, pl.ds(0, used)], dst_ref=xrecv.at[t, s, me, pl.ds(0, used)], send_sem=x_send.at[s, i],
             recv_sem=x_recv.at[t, s, i],
             device_id={"net": peer // lines, "line": lax.rem(peer, lines)}, device_id_type=MESH,
         )

time: 244 us -> 239 us (0.980)
  Pallas kernels: 243 us -> 238 us
    pallas_call x1, Pallas kernels: 241 us -> 236 us  [on_device(): pl.pallas_call(functools.partial(kernel, lines, nets), out_shape=(jax.Sha...]
where the time goes in v3:
time: 239 us
  Pallas kernels  238 us (100%)
    pallas_call x1, Pallas kernels, on_device(): pl.pallas_call(functools.partial(kernel, lines, nets), out_shape=(jax.Sha...  236 us

profile of v3, /device:TPU:1, one launch (start us, length us, event | category | flops | bytes accessed | tf_op | source)
XLA Modules:
  0.0 238.9 jit_solution(17287099779858068152)
XLA Ops:
  0.6 236.2 %network.1 = (f32[96,512]{1,0:T(8,128)}, f32[3,96,512]{2,1,0:T(8,128)}) custom-call(f32[96,512]{1,0:T(8,128)} %bitcast.18, f32[3,1,512]{2,1,0:T(1,128)} %source_ref.1, s32[1,96]{1,0:T(1,128)} %bitcast.24, f32[1,96]{1,0:T(1,128)} %bitcast.25, s32[3,1,512]{2,1,0:T(1,128)} %bitcast.23, s32[1,512]{1,0:T(1,128)} %live_ref.1, s32[1,512]{1,0:T(1,128)} %partner_ref.1, ...), custom_call_target="tpu_custom_call" | custom-call | tf_op jit(solution)/shard_map/network/pallas_call | solution.py:698
  236.9 2.1 hand_over.1
